TPU v7x, 32 devices: a whole 2x2x4 slice. The times are simulated.
32 devices in a mesh: dp: 2 (over x), cp: 16 (over z, y, core).
Axes of the slice: x: 2, y: 2, z: 4, core: 2. Of those that a mesh axis runs over, the one named last changes fastest.
Arguments:
- image: bfloat16 [2, 6144, 3072], P('dp', 'cp'), parts along dimension 0
- text: bfloat16 [2, 256, 3072], P('dp'), parts along dimension 0
- cond_vec: bfloat16 [2, 3072], P('dp'), parts along dimension 0
- image_ids: int32 [12288, 3], P(('dp', 'cp')), parts along dimension 0
- img_w_mod: bfloat16 [3072, 18432], replicated
- img_b_mod: bfloat16 [18432], replicated
- img_w_qkv: bfloat16 [3072, 9216], replicated
- img_b_qkv: bfloat16 [9216], replicated
- img_q_gain: bfloat16 [128], replicated
- img_k_gain: bfloat16 [128], replicated
- img_w_proj: bfloat16 [3072, 3072], replicated
- img_b_proj: bfloat16 [3072], replicated
- img_w_fc1: bfloat16 [3072, 12288], replicated
- img_b_fc1: bfloat16 [12288], replicated
- img_w_fc2: bfloat16 [12288, 3072], replicated
- img_b_fc2: bfloat16 [3072], replicated
- txt_w_mod: bfloat16 [3072, 18432], replicated
- txt_b_mod: bfloat16 [18432], replicated
- txt_w_qkv: bfloat16 [3072, 9216], replicated
- txt_b_qkv: bfloat16 [9216], replicated
- txt_q_gain: bfloat16 [128], replicated
- txt_k_gain: bfloat16 [128], replicated
- txt_w_proj: bfloat16 [3072, 3072], replicated
- txt_b_proj: bfloat16 [3072], replicated
- txt_w_fc1: bfloat16 [3072, 12288], replicated
- txt_b_fc1: bfloat16 [12288], replicated
- txt_w_fc2: bfloat16 [12288, 3072], replicated
- txt_b_fc2: bfloat16 [3072], replicated
Outputs:
- output 1: bfloat16 [2, 6144, 3072], P('dp', 'cp'), parts along dimension 0
- output 2: bfloat16 [2, 256, 3072], P('dp'), parts along dimension 0
There are 2 independent parts. A program takes and returns all parts, laid end to end along the dimension named above; an argument that names none is the same for every part.
All inputs are finite; a program needn't handle non-finite values.
Results may differ from a plain program's by a relative error of at most 0.00561117.
Values are sent between devices in bfloat16 or wider.
A program may use at most 2.75 GiB of HBM per device.

v0:
```python
import functools

import jax
import jax.numpy as jnp
import numpy as np
from jax import lax
from jax.experimental import pallas as pl
from jax.experimental.pallas import tpu as pltpu
from jax.sharding import PartitionSpec as P

EPS = 1e-6
THETA = 10000.0
F32 = jnp.float32
BF16 = jnp.bfloat16
HD = 128
NCHIP = 8
NDEV = 16
VM = pl.BlockSpec(memory_space=pltpu.VMEM)
ANY = pl.BlockSpec(memory_space=pl.ANY)
MESH = pl.DeviceIdType.MESH
VMEM_LIMIT = 67043328


def dot(a, b):
    return jnp.dot(a, b, preferred_element_type=F32)


def dot_t(a, b):
    return lax.dot_general(a, b, (((1,), (1,)), ((), ())), preferred_element_type=F32)


def lane_row(b_ref, start, n):
    return b_ref[pl.ds(start, n)].astype(F32).reshape(1, n)


def ln_mod_rows(x, scale1p, shift):
    xf = x.astype(F32)
    mean = jnp.mean(xf, axis=-1, keepdims=True)
    cent = xf - mean
    var = jnp.mean(cent * cent, axis=-1, keepdims=True)
    return scale1p * (cent * lax.rsqrt(var + EPS)) + shift


KINDS = (1, 2, 0)


def main_kernel(cfg, x_hbm, xt_hbm, cond_ref, wmi_hbm, wmt_hbm, wi_hbm, wt_hbm, bmi_ref, bmt_ref, bi_ref, bt_ref,
                qg_ref, kg_ref, tqg_ref, tkg_ref, pos_ref, om_ref,
                o_hbm, ot_ref, g2,
                w, xs, xm, xt, kn, kf, km, vn, vf, vm, qn, qf, qm, kb, vb, qb, posm, cos_t, se_t, so_t, cos_m, se_m, so_m,
                mi, mt, g1, mine1, mine2, s0, s1, mx0, mx1, ost, otmp,
                xsem, wsem, msend, mrecv, gsend, grecv, ssem, rsem, fssem, frsem, ossem, orsem):
    tok, txt, d_in, heads, ck, mx = cfg
    nu = tok - mx
    hd_all = heads * HD
    nj = heads // NCHIP
    quad = 4
    wide = quad * HD
    half = tok * NCHIP
    me = lax.axis_index("cp")
    chip, core = me // 2, me % 2
    zh, cl = chip // quad, chip % quad
    sib = chip * 2 + (1 - core)
    mirror_chip = lax.rem(chip + quad, NCHIP)

    def dev(c):
        return {"cp": c * 2 + core}

    barrier = pltpu.get_barrier_semaphore()
    for r in range(1, NDEV):
        pl.semaphore_signal(barrier, inc=1, device_id={"cp": lax.rem(me + r, NDEV)}, device_id_type=MESH)
    load_x = pltpu.make_async_copy(x_hbm, xs, xsem.at[0])
    load_t = pltpu.make_async_copy(xt_hbm, xt, xsem.at[1])

    def x_copy():
        return pltpu.make_async_remote_copy(
            src_ref=x_hbm.at[pl.ds(nu, mx), :], dst_ref=xm, send_sem=msend.at[0], recv_sem=mrecv.at[0],
            device_id=dev(mirror_chip), device_id_type=MESH)

    def pos_copy():
        return pltpu.make_async_remote_copy(
            src_ref=pos_ref.at[pl.ds(nu, mx), :], dst_ref=posm, send_sem=msend.at[1], recv_sem=mrecv.at[1],
            device_id=dev(mirror_chip), device_id_type=MESH)

    mc = 2 * d_in // NDEV

    def tile_copy(what, a, b, slot):
        if what == "mod":
            ref = (wmi_hbm, wmt_hbm)[a]
            off = me * mc if b < 0 else 2 * d_in + me * 2 * mc + b * mc
            return [pltpu.make_async_copy(ref.at[:, pl.ds(pl.multiple_of(off, 128), mc)], w.at[slot, :, pl.ds(0, mc)], wsem.at[slot, 0])]
        if what == "txt":
            return [pltpu.make_async_copy(
                wt_hbm.at[:, pl.ds(pl.multiple_of(a * hd_all + (j * NCHIP + chip) * HD, HD), HD)],
                w.at[slot, :, pl.ds(j * HD, HD)], wsem.at[slot, j]) for j in range(nj)]
        kind, side = a
        off = kind * hd_all + b * NCHIP * HD + (zh if side == 0 else 1 - zh) * wide
        return [pltpu.make_async_copy(wi_hbm.at[:, pl.ds(pl.multiple_of(off, wide), wide)], w.at[slot], wsem.at[slot, 0])]

    def start(*a):
        for c in tile_copy(*a):
            c.start()

    def wait(*a):
        for c in tile_copy(*a):
            c.wait()
        return a[-1]

    def start_own(j, p):
        start("img", (KINDS[p // 2], p % 2), j, (2 + p) % 3)

    def start_txt(t):
        start("txt", KINDS[t], None, (2 + t) % 3)

    def start_mir(j, i):
        start("img", (KINDS[i], 0), j, (2 + i) % 3)

    def start_mod2(t):
        start("mod", t // 2, t % 2, (2 + t) % 3)

    start("mod", 0, -1, 0)
    start("mod", 1, -1, 1)
    load_x.start()
    load_t.start()

    c = cond_ref[...].astype(F32)
    act = (c * jax.nn.sigmoid(c)).astype(BF16)
    act = jnp.broadcast_to(act, (16, d_in))
    per = mc // 128

    def mod_rows(slot, buf, row):
        r = dot(act, w[slot, :, 0:mc])
        for i in range(per):
            buf[row + i:row + i + 1, :] = r[0:1, i * 128:(i + 1) * 128]

    def spread(buf, dst, k):
        return [pltpu.make_async_remote_copy(
            src_ref=buf, dst_ref=dst.at[me], send_sem=gsend.at[k, r], recv_sem=grecv.at[k, r],
            device_id={"cp": lax.rem(me + r, NDEV)}, device_id_type=MESH) for r in range(1, NDEV)]

    mine1[...] = jnp.zeros_like(mine1)
    start_own(0, 0)
    mod_rows(wait("mod", 0, -1, 0), mine1, 0)
    start_own(0, 1)
    mod_rows(wait("mod", 1, -1, 1), mine1, per)
    pl.semaphore_wait(barrier, NDEV - 1)
    gath1 = spread(mine1, g1, 0)
    for cp in gath1:
        cp.start()
    pos_copy().start()
    x_copy().start()
    g1[me] = mine1[...]

    def tables(pos, n, cos_t, se_t, so_t):
        ang = pos.astype(F32) * om_ref[...]
        odd = lax.rem(lax.broadcasted_iota(jnp.int32, ang.shape, 1), 2) == 1
        sin = jnp.sin(ang)
        cos_t[0:n, :] = jnp.cos(ang)
        se_t[0:n, :] = jnp.where(odd, 0.0, -sin)
        so_t[0:n, :] = jnp.where(odd, sin, 0.0)

    tables(pos_ref[...], tok, cos_t, se_t, so_t)
    for b_ref, m in ((bmi_ref, mi), (bmt_ref, mt)):
        for k in range(2):
            m[k:k + 1, :] = lane_row(b_ref, k * d_in, d_in)
    for cp in gath1:
        cp.wait()
    for b, m in ((0, mi), (1, mt)):
        for dv in range(NDEV):
            for r in range(per):
                col = (dv * per + r) * 128
                at = (slice(col // d_in, col // d_in + 1), slice(col % d_in, col % d_in + 128))
                m[at] = m[at] + g1[dv, b * per + r:b * per + r + 1, :]

    rb = 16

    def ln_rows(ref, m_ref, n):
        shift = m_ref[0:1, :]
        scale = 1.0 + m_ref[1:2, :]

        def body(i, carry):
            sl = pl.ds(pl.multiple_of(i * rb, rb), rb)
            ref[sl, :] = ln_mod_rows(ref[sl, :], scale, shift).astype(BF16)
            return carry
        lax.fori_loop(0, n // rb, body, 0)

    def norm_rope(y, gain, tabs):
        ms = jnp.mean(y * y, axis=-1, keepdims=True)
        y = y * lax.rsqrt(ms + EPS) * gain
        if tabs is not None:
            n = y.shape[0]
            y = y * tabs[0][0:n, :] + pltpu.roll(y, HD - 1, 1) * tabs[1][0:n, :] + pltpu.roll(y, 1, 1) * tabs[2][0:n, :]
        return y

    def place(kind, s_chip, row, n, j):
        if kind == 0:
            return qb.at[j, pl.ds(pl.multiple_of(txt + s_chip * tok + row, 128), n)]
        at = pl.multiple_of(txt + core * half + s_chip * tok + row, 128)
        return kb.at[j, pl.ds(at, n)] if kind == 1 else vb.at[j, :, pl.ds(at, n)]

    def qkv_copy(kind, ty, j, src_cl, src_zh, dst_cl, idx):
        buf = ((qn, qf, qm), (kn, kf, km), (vn, vf, vm))[kind][ty]
        n = (tok, nu, mx)[ty]
        s_chip = src_zh * quad + src_cl
        tgt = (1 - src_zh if ty == 1 else src_zh) * quad + dst_cl
        if ty == 2:
            dst = place(kind, lax.rem(s_chip + quad, NCHIP), nu, n, j)
        else:
            dst = place(kind, s_chip, 0, n, j)
        return pltpu.make_async_remote_copy(
            src_ref=buf.at[j * quad + dst_cl], dst_ref=dst, send_sem=ssem.at[kind, ty, j, idx[0]],
            recv_sem=rsem.at[kind, ty, j, idx[1]], device_id=dev(tgt), device_id_type=MESH)

    def out_copies(kind, ty, j):
        if ty == 1:
            return [qkv_copy(kind, 1, j, cl, zh, c, (c, cl)) for c in range(quad)]
        return [qkv_copy(kind, ty, j, cl, zh, lax.rem(cl + r, quad), (r, r)) for r in range(1, quad)]

    def in_copies(kind, ty, j):
        if ty == 1:
            return [qkv_copy(kind, 1, j, c, 1 - zh, cl, (c, c)) for c in range(quad)]
        return [qkv_copy(kind, ty, j, lax.rem(cl + quad - r, quad), zh, cl, (r, r)) for r in range(1, quad)]

    def own_copy(kind, ty, j):
        buf = ((qn, qf, qm), (kn, kf, km), (vn, vf, vm))[kind][ty]
        n = (tok, nu, mx)[ty]
        dst = place(kind, mirror_chip, nu, n, j) if ty == 2 else place(kind, chip, 0, n, j)
        dst[...] = buf[j * quad + cl]

    def make(kind, ty, j, slot):
        src = xm if ty == 2 else xs
        n = (tok, nu, mx)[ty]
        buf = ((qn, qf, qm), (kn, kf, km), (vn, vf, vm))[kind][ty]

        def cols(p, carry):
            col = pl.multiple_of(p * 2 * HD, 2 * HD)
            boff = kind * hd_all + j * NCHIP * HD + (1 - zh if ty == 1 else zh) * wide + col
            y2 = dot(src[0:n, :], w[slot, :, pl.ds(col, 2 * HD)]) + lane_row(bi_ref, pl.multiple_of(boff, 256), 2 * HD)
            for hh in range(2):
                y = y2[:, hh * HD:(hh + 1) * HD]
                if kind == 2:
                    buf[j * quad + 2 * p + hh] = y.T.astype(BF16)
                else:
                    gain = (qg_ref, kg_ref)[kind][...].astype(F32).reshape(1, HD)
                    buf[j * quad + 2 * p + hh] = norm_rope(y, gain, (cos_m, se_m, so_m) if ty == 2 else (cos_t, se_t, so_t)).astype(BF16)
            return carry
        lax.fori_loop(0, 2, cols, 0)

    load_x.wait()
    ln_rows(xs, mi, tok)

    last = nj - 1
    mir_after = min(1, last)

    def text_rows():
        load_t.wait()
        ln_rows(xt, mt, txt)
        for t, kind in enumerate(KINDS):
            if t == 0:
                start_txt(2)
            elif nj > 1:
                start_own(1, t - 1)
            else:
                start_mir(0, t - 1)
            slot = wait("txt", kind, None, (2 + t) % 3)
            y3 = dot(xt[...], w[slot, :, 0:nj * HD])
            for j in range(nj):
                pair0 = kind * hd_all + (j * NCHIP + chip - lax.rem(chip, 2)) * HD
                b2 = lane_row(bt_ref, pl.multiple_of(pair0, 256), 2 * HD)
                y = y3[:, j * HD:(j + 1) * HD] + jnp.where(lax.rem(chip, 2) == 0, b2[:, 0:HD], b2[:, HD:2 * HD])
                if kind == 2:
                    vb[j, :, 0:txt] = y.T.astype(BF16)
                else:
                    gain = (tqg_ref, tkg_ref)[kind][...].astype(F32).reshape(1, HD)
                    (qb, kb)[kind][j, 0:txt] = norm_rope(y, gain, None).astype(BF16)

    def mirror_rows():
        pos_copy().wait_recv()
        tables(posm[...], mx, cos_m, se_m, so_m)
        x_copy().wait_recv()
        ln_rows(xm, mi, mx)

        lax.fori_loop(0, nj, mir_pass, 0)

    def mir_pass(j, carry):
        for i, kind in enumerate(KINDS):
            if i == 0:
                start_mir(j, 2)
            else:
                @pl.when(j < nj - 1)
                def _():
                    start_mir(j + 1, i - 1)

                @pl.when(j == nj - 1)
                def _():
                    if mir_after < last:
                        start_own(mir_after + 1, i - 1)
                    else:
                        start_mod2(i - 1)
            slot = wait("img", (kind, 0), j, (2 + i) % 3)
            make(kind, 2, j, slot)
            for cp in out_copies(kind, 2, j):
                cp.start()
            own_copy(kind, 2, j)
        return carry

    def after_own(j, p):
        @pl.when(j == 0)
        def _():
            start_txt(p)

        if mir_after > 0:
            @pl.when(j == mir_after)
            def _():
                start_mir(0, p)

        @pl.when((j > mir_after) & (j < last))
        def _():
            start_own(j + 1, p)

        if last > mir_after:
            @pl.when(j == last)
            def _():
                start_mod2(p)

    def own_pass(j, carry):
        for p in range(6):
            kind, side = KINDS[p // 2], p % 2
            if p + 2 < 6:
                start_own(j, p + 2)
            else:
                after_own(j, p - 4)
            slot = wait("img", (kind, side), j, (2 + p) % 3)
            make(kind, side, j, slot)
            for cp in out_copies(kind, side, j):
                cp.start()
            if side == 0:
                own_copy(kind, 0, j)

        pl.when(j == 0)(text_rows)
        pl.when(j == mir_after)(mirror_rows)
        return carry
    lax.fori_loop(0, nj, own_pass, 0)

    mine2[...] = jnp.zeros_like(mine2)
    for t in range(4):
        if t + 2 < 4:
            start_mod2(t + 2)
        mod_rows(wait("mod", t // 2, t % 2, (2 + t) % 3), mine2, t * per)
    gath2 = spread(mine2, g2, 1)
    for cp in gath2:
        cp.start()
    g2[me] = mine2[...]

    scale2 = (HD ** -0.5) * 1.4426950408889634
    keys = txt + 2 * half
    nchunk = keys // ck
    qt = 256
    ntile = (txt + half) // qt
    group = 2 * tok // qt
    ngroup = NCHIP // 2

    def to_sibling(kind, j):
        ref = (kb.at[j, pl.ds(pl.multiple_of(txt + core * half, 128), half)] if kind == 1
               else vb.at[j, :, pl.ds(pl.multiple_of(txt + core * half, 128), half)])
        return pltpu.make_async_remote_copy(
            src_ref=ref, dst_ref=ref, send_sem=fssem.at[kind - 1, j], recv_sem=frsem.at[kind - 1, j],
            device_id={"cp": sib}, device_id_type=MESH)

    def collect(j):
        for kind in KINDS:
            for ty in range(3):
                for cp in in_copies(kind, ty, j):
                    cp.wait_recv()
            if kind != 0:
                to_sibling(kind, j).start()

    def tile_start(t):
        g = (t - 1) // group
        plane = lax.rem(chip // 2 + 1 + g, ngroup)
        row = txt + plane * (2 * tok) + lax.rem(t - 1, group) * qt
        return pl.multiple_of(jnp.where(t == 0, 0, row), 128)

    def qk(j, q, i, s_ref, mxv):
        sl = pl.ds(pl.multiple_of(i * ck, ck), ck)
        s = dot_t(kb[j, sl], q)
        s_ref[sl, :] = s
        return jnp.maximum(mxv, jnp.max(s.reshape(ck // 8, 8, qt), axis=0))

    def sm(j, i, s_ref, m, lsum, acc):
        sl = pl.ds(pl.multiple_of(i * ck, ck), ck)
        p = jnp.exp2((s_ref[sl, :] - m) * scale2)
        lsum = lsum + jnp.sum(p.reshape(ck // 8, 8, qt), axis=0)
        acc = acc + dot(vb[j, :, sl], p.astype(BF16))
        return lsum, acc

    def new_max():
        return jnp.full((8, qt), -jnp.inf, F32)

    def o_remote(j, c_src, c_dst):
        src = ost.at[j, pl.ds(pl.multiple_of(c_dst * tok, 128), tok)]
        dst = o_hbm.at[:, pl.ds(pl.multiple_of((j * NCHIP + c_src) * HD, HD), HD)]
        return pltpu.make_async_remote_copy(
            src_ref=src, dst_ref=dst, send_sem=ossem.at[j, c_dst], recv_sem=orsem.at[j, c_src],
            device_id=dev(c_dst), device_id_type=MESH)

    def o_local(j):
        src = ost.at[j, pl.ds(pl.multiple_of(chip * tok, 128), tok)]
        dst = o_hbm.at[:, pl.ds(pl.multiple_of((j * NCHIP + chip) * HD, HD), HD)]
        return pltpu.make_async_copy(src, dst, ossem.at[j, chip])

    def o_send(j, g):
        plane = lax.rem(chip // 2 + 1 + g, ngroup)
        for y in range(2):
            c = plane * 2 + y

            @pl.when(c != chip)
            def _():
                o_remote(j, chip, c).start()

            @pl.when(c == chip)
            def _():
                o_local(j).start()

    def finish(j, t, lsum, acc):
        tot = jnp.sum(lsum, axis=0, keepdims=True)
        o = (acc / tot).T.astype(BF16)

        @pl.when(t == 0)
        def _():
            otmp[...] = o
            ot_ref[j] = otmp[pl.ds(pl.multiple_of(core * (txt // 2), 8), txt // 2), :]

        @pl.when(t > 0)
        def _():
            ost[j, pl.ds(pl.multiple_of(tile_start(t) - txt, 128), qt)] = o

            @pl.when(lax.rem(t, group) == 0)
            def _():
                o_send(j, t // group - 1)

    def pair(j, t, s_cur, mx_cur, s_nxt, mx_nxt, has_next):
        m = jnp.max(mx_cur[...], axis=0, keepdims=True)
        lsum = jnp.zeros((8, qt), F32)
        acc = jnp.zeros((HD, qt), F32)
        if has_next:
            q = qb[j, pl.ds(tile_start(t + 1), qt)]

            def body(i, carry):
                lsum, acc, mxv = carry
                mxv = qk(j, q, i, s_nxt, mxv)
                lsum, acc = sm(j, i, s_cur, m, lsum, acc)
                return lsum, acc, mxv
            lsum, acc, mxv = lax.fori_loop(0, nchunk, body, (lsum, acc, new_max()))
            mx_nxt[...] = mxv
        else:
            def body(i, carry):
                return sm(j, i, s_cur, m, *carry)
            lsum, acc = lax.fori_loop(0, nchunk, body, (lsum, acc))
        finish(j, t, lsum, acc)

    collect(0)

    def head(j, carry):
        for kind in (1, 2):
            to_sibling(kind, j).wait()
        q = qb[j, 0:qt]

        def first(i, mxv):
            return qk(j, q, i, s0, mxv)
        mx0[...] = lax.fori_loop(0, nchunk, first, new_max())

        def two(i, carry):
            pair(j, 2 * i, s0, mx0, s1, mx1, True)
            pair(j, 2 * i + 1, s1, mx1, s0, mx0, True)
            return carry
        lax.fori_loop(0, (ntile - 1) // 2, two, 0)
        if nj > 1:
            @pl.when(j < nj - 1)
            def _():
                collect(j + 1)
        pair(j, jnp.int32(ntile - 1), s0, mx0, s1, mx1, False)
        return carry
    lax.fori_loop(0, nj, head, 0)

    for cp in gath2:
        cp.wait()
    x_copy().wait_send()
    pos_copy().wait_send()

    def drain(j, carry):
        for kind in KINDS:
            for ty in range(3):
                for cp in out_copies(kind, ty, j):
                    cp.wait_send()
        o_local(j).wait()
        for r in range(1, NCHIP):
            c = lax.rem(chip + r, NCHIP)
            o_remote(j, chip, c).wait_send()
            o_remote(j, c, chip).wait_recv()
        return carry
    lax.fori_loop(0, nj, drain, 0)


def attention(image, text, cond_vec, wm_img, wm_txt, w_img, w_txt, flat, pos, omega):
    tok, d_in = image.shape
    txt = text.shape[0]
    hd_all = w_img.shape[1] // 3
    heads = hd_all // HD
    nj = heads // NCHIP
    half = tok * NCHIP
    keys = txt + 2 * half
    ck = 3200
    mx = 2 * tok // 3
    nu = tok - mx
    cfg = (tok, txt, d_in, heads, ck, mx)
    dma = pltpu.SemaphoreType.DMA
    flops = 2 * tok * d_in * 3 * hd_all + 4 * nj * HD * (half + txt) * keys
    per = 2 * d_in // NDEV // 128
    r1, r2 = -(-2 * per // 8) * 8, -(-4 * per // 8) * 8
    row_sets = [pltpu.VMEM((nj * 4, n, HD), BF16) for n in (tok, nu, mx)]
    col_sets = [pltpu.VMEM((nj * 4, HD, n), BF16) for n in (tok, nu, mx)]
    table = pltpu.VMEM((tok, 128), F32)
    return pl.pallas_call(
        functools.partial(main_kernel, cfg),
        out_shape=(jax.ShapeDtypeStruct((tok, hd_all), BF16), jax.ShapeDtypeStruct((nj, txt // 2, HD), BF16),
                   jax.ShapeDtypeStruct((NDEV, r2, 128), F32)),
        in_specs=[ANY, ANY, VM, ANY, ANY, ANY, ANY] + [VM] * 10,
        out_specs=(ANY, VM, VM),
        scratch_shapes=[
            pltpu.VMEM((3, d_in, 4 * HD), BF16),
            pltpu.VMEM((tok, d_in), BF16), pltpu.VMEM((mx, d_in), BF16), pltpu.VMEM((txt, d_in), BF16),
            *row_sets, *col_sets, *row_sets,
            pltpu.VMEM((nj, keys, HD), BF16), pltpu.VMEM((nj, HD, keys), BF16), pltpu.VMEM((nj, txt + half, HD), BF16),
            pltpu.VMEM((mx, 128), BF16), table, table, table, *[pltpu.VMEM((mx, 128), F32)] * 3,
            pltpu.VMEM((2, d_in), F32), pltpu.VMEM((2, d_in), F32),
            pltpu.VMEM((NDEV, r1, 128), F32), pltpu.VMEM((r1, 128), F32), pltpu.VMEM((r2, 128), F32),
            pltpu.VMEM((keys, 256), F32), pltpu.VMEM((keys, 256), F32), pltpu.VMEM((8, 256), F32), pltpu.VMEM((8, 256), F32),
            pltpu.VMEM((nj, half, HD), BF16), pltpu.VMEM((txt, HD), BF16),
            dma((2,)), dma((3, max(nj, 1))), dma((2,)), dma((2,)), dma((2, NDEV)), dma((2, NDEV)),
            dma((3, 3, nj, 4)), dma((3, 3, nj, 4)), dma((2, nj)), dma((2, nj)), dma((nj, NCHIP)), dma((nj, NCHIP)),
        ],
        compiler_params=pltpu.CompilerParams(collective_id=1, has_side_effects=True, vmem_limit_bytes=VMEM_LIMIT),
        cost_estimate=pl.CostEstimate(flops=flops, bytes_accessed=3 * d_in * 3 * hd_all, transcendentals=0),
        name="attn",
    )(image, text, cond_vec, wm_img, wm_txt, w_img, w_txt, *flat, pos, omega)


def gelu(x):
    return x * (0.5 * (1.0 + jnp.tanh(0.7978845608028654 * (x + 0.044715 * (x * x * x)))))


def out_kernel(cfg, o_hbm, x_hbm, xt_hbm, ot_ref, g2_ref, bmi_ref, bmt_ref, bp_ref, tbp_ref, b1_ref, tb1_ref, b2_ref, tb2_ref, wp_hbm, w1_hbm, w2_hbm, twp_hbm, tw1_hbm, tw2_hbm,
               out_ref, tout_ref, mi_ref, mt_ref,
               wa, wb, wc, o, x, h, z, acc, a0, a1, o_t, x_t, h_t, z_t, a_t, part, rs, row,
               asem, bsem, csem, lsem, ossem, orsem, pssem, prsem, rssem, rrsem, fssem, frsem):
    tok, txt, d, ff, k1, k2 = cfg
    me = lax.axis_index("cp")
    chip, core = me // 2, me % 2
    sib = chip * 2 + (1 - core)
    rows = txt // 2
    piece = rows // NCHIP
    nb = wa.shape[2]
    na = wa.shape[0]
    np_ = d // nb
    nf = ff // nb
    ft = ff // NCHIP
    nt = ft // nb
    nj = ot_ref.shape[0]

    def dev(c):
        return {"cp": c * 2 + core}

    off = pl.multiple_of(chip * ft, nb)

    def start_a(p):
        slot = lax.rem(p, na)

        @pl.when(p < np_)
        def _():
            pltpu.make_async_copy(wp_hbm.at[:, pl.ds(pl.multiple_of(p * nb, nb), nb)], wa.at[slot], asem.at[slot]).start()

        @pl.when((p >= np_) & (p < np_ + nf))
        def _():
            pltpu.make_async_copy(w1_hbm.at[:, pl.ds(pl.multiple_of((p - np_) * nb, nb), nb)], wa.at[slot], asem.at[slot]).start()

    def start_b(p):
        slot = lax.rem(p, na)

        @pl.when(p < nf)
        def _():
            pltpu.make_async_copy(w2_hbm.at[pl.ds(pl.multiple_of(p * nb, nb), nb), :], wb.at[slot], bsem.at[slot]).start()

    def c_fc2(p, slot):
        return pltpu.make_async_copy(tw2_hbm.at[pl.ds(off, ft), pl.ds(pl.multiple_of(p * nb, nb), nb)],
                                     wc.at[slot, pl.ds(0, ft), :], csem.at[slot])

    def start_c(p):
        slot = lax.rem(p, na)

        @pl.when(p < np_)
        def _():
            pltpu.make_async_copy(twp_hbm.at[:, pl.ds(pl.multiple_of(p * nb, nb), nb)], wc.at[slot], csem.at[slot]).start()

        @pl.when((p >= np_) & (p < np_ + nt))
        def _():
            pltpu.make_async_copy(tw1_hbm.at[:, pl.ds(pl.multiple_of(off + (p - np_) * nb, nb), nb)], wc.at[slot], csem.at[slot]).start()

        @pl.when((p >= np_ + nt) & (p < np_ + nt + np_))
        def _():
            c_fc2(p - np_ - nt, slot).start()

    def get_a(p):
        start_a(p + na - 1)
        slot = lax.rem(p, na)
        pltpu.make_async_copy(w1_hbm.at[:, 0:nb], wa.at[slot], asem.at[slot]).wait()
        return slot

    def get_b(p):
        start_b(p + na - 1)
        slot = lax.rem(p, na)
        pltpu.make_async_copy(w2_hbm.at[0:nb, :], wb.at[slot], bsem.at[slot]).wait()
        return slot

    def get_c(p, fc2=False):
        start_c(p + na - 1)
        slot = lax.rem(p, na)
        if fc2:
            c_fc2(0, slot).wait()
        else:
            pltpu.make_async_copy(w1_hbm.at[:, 0:nb], wc.at[slot], csem.at[slot]).wait()
        return slot

    load_o = pltpu.make_async_copy(o_hbm, o, lsem.at[0])
    load_x = pltpu.make_async_copy(x_hbm, x, lsem.at[1])
    load_t = pltpu.make_async_copy(xt_hbm.at[pl.ds(pl.multiple_of(core * rows, 8), rows), :], x_t, lsem.at[2])
    load_o.start()
    start_a(jnp.int32(0))
    load_x.start()
    for p in range(1, na - 1):
        start_a(jnp.int32(p))
    load_t.start()
    for p in range(na - 1):
        start_b(jnp.int32(p))
    for p in range(na - 1):
        start_c(jnp.int32(p))

    barrier = pltpu.get_barrier_semaphore()
    for r in range(1, NCHIP):
        pl.semaphore_signal(barrier, inc=1, device_id=dev(lax.rem(chip + r, NCHIP)), device_id_type=MESH)
    pl.semaphore_signal(barrier, inc=1, device_id={"cp": sib}, device_id_type=MESH)
    pl.semaphore_wait(barrier, NCHIP)

    def o_copy(j, r, c_src, c_dst):
        return pltpu.make_async_remote_copy(
            src_ref=ot_ref.at[j], dst_ref=o_t.at[:, pl.ds(pl.multiple_of((j * NCHIP + c_src) * HD, HD), HD)],
            send_sem=ossem.at[j, r], recv_sem=orsem.at[j, r], device_id=dev(c_dst), device_id_type=MESH)

    for j in range(nj):
        for r in range(1, NCHIP):
            o_copy(j, r, chip, lax.rem(chip + r, NCHIP)).start()
        o_t[:, pl.ds(pl.multiple_of((j * NCHIP + chip) * HD, HD), HD)] = ot_ref[j]

    per = 4 * d // NDEV // 128
    for b, (b_ref, m) in enumerate(((bmi_ref, mi_ref), (bmt_ref, mt_ref))):
        for k in range(2, 6):
            m[k:k + 1, :] = lane_row(b_ref, k * d, d)
        for dv in range(NDEV):
            for r in range(per):
                col = 2 * d + (dv * per + r) * 128
                at = (slice(col // d, col // d + 1), slice(col % d, col % d + 128))
                m[at] = m[at] + g2_ref[dv, b * per + r:b * per + r + 1, :]

    load_o.wait()
    load_x.wait()

    def proj(p, carry):
        slot = get_a(p)
        sl = pl.ds(pl.multiple_of(p * nb, nb), nb)
        y = dot(o[...], wa[slot]) + lane_row(bp_ref, pl.multiple_of(p * nb, nb), nb)
        h[:, sl] = x[:, sl].astype(F32) + mi_ref[2:3, sl] * y
        return carry
    lax.fori_loop(0, np_, proj, 0)

    def ln2(src, dst, m_ref, n):
        shift, scale = m_ref[3:4, :], 1.0 + m_ref[4:5, :]
        rb = 16

        def body(i, carry):
            r = pl.ds(pl.multiple_of(i * rb, rb), rb)
            dst[r, :] = ln_mod_rows(src[r, :], scale, shift).astype(BF16)
            return carry
        lax.fori_loop(0, n // rb, body, 0)

    ln2(h, z, mi_ref, tok)
    acc[...] = jnp.broadcast_to(lane_row(b2_ref, 0, d), acc.shape)

    def tproj(p, carry):
        slot = get_c(p)
        sl = pl.ds(pl.multiple_of(p * nb, nb), nb)
        y = dot(o_t[...], wc[slot]) + lane_row(tbp_ref, pl.multiple_of(p * nb, nb), nb)
        h_t[:, sl] = x_t[:, sl].astype(F32) + mt_ref[2:3, sl] * y
        return carry

    def tfc1(p, carry):
        slot = get_c(np_ + p)
        col = pl.multiple_of(p * nb, nb)
        y = dot(z_t[...], wc[slot]) + lane_row(tb1_ref, pl.multiple_of(off + col, nb), nb)
        a_t[:, pl.ds(col, nb)] = gelu(y).astype(BF16)
        return carry

    def tfc2(p, carry):
        slot = get_c(np_ + nt + p, True)
        part[:, pl.ds(pl.multiple_of(p * nb, nb), nb)] = dot(a_t[...], wc[slot, 0:ft, :])
        return carry

    def p_copy(r, c_src, c_dst):
        return pltpu.make_async_remote_copy(
            src_ref=part.at[pl.ds(pl.multiple_of(c_dst * piece, 8), piece), :], dst_ref=rs.at[c_src],
            send_sem=pssem.at[r], recv_sem=prsem.at[r], device_id=dev(c_dst), device_id_type=MESH)

    mine = pl.ds(pl.multiple_of(chip * piece, 8), piece)

    def text0():
        load_t.wait()
        for j in range(nj):
            for r in range(1, NCHIP):
                o_copy(j, r, lax.rem(chip + NCHIP - r, NCHIP), chip).wait_recv()
        lax.fori_loop(0, np_ // 2, tproj, 0)

    def text1():
        lax.fori_loop(np_ // 2, np_, tproj, 0)

    def text2():
        ln2(h_t, z_t, mt_ref, rows)
        lax.fori_loop(0, nt, tfc1, 0)

    def text3():
        lax.fori_loop(0, np_, tfc2, 0)
        for r in range(1, NCHIP):
            p_copy(r, chip, lax.rem(chip + r, NCHIP)).start()
        rs[chip] = part[mine, :]

    def r_copy(r, c_src, c_dst):
        return pltpu.make_async_remote_copy(
            src_ref=row, dst_ref=tout_ref.at[pl.ds(pl.multiple_of(core * rows + c_src * piece, 8), piece), :],
            send_sem=rssem.at[r], recv_sem=rrsem.at[r], device_id=dev(c_dst), device_id_type=MESH)

    def text4():
        for r in range(1, NCHIP):
            p_copy(r, lax.rem(chip + NCHIP - r, NCHIP), chip).wait_recv()
        tot = rs[0]
        for c in range(1, NCHIP):
            tot = tot + rs[c]
        y = h_t[mine, :] + mt_ref[5:6, :] * (tot + lane_row(tb2_ref, 0, d))
        row[...] = y.astype(BF16)
        for r in range(1, NCHIP):
            r_copy(r, chip, lax.rem(chip + r, NCHIP)).start()
        tout_ref[pl.ds(pl.multiple_of(core * rows + chip * piece, 8), piece), :] = row[...]

    def mlp(i, a_new, a_old):
        slot_b = get_b(i - 1)
        slot_a = get_a(np_ + i)
        a_new[...] = gelu(dot(z[...], wa[slot_a]) + lane_row(b1_ref, pl.multiple_of(i * nb, nb), nb)).astype(BF16)
        acc[...] += dot(a_old[...], wb[slot_b])

    slot = get_a(jnp.int32(np_))
    a0[...] = gelu(dot(z[...], wa[slot]) + lane_row(b1_ref, 0, nb)).astype(BF16)

    def two(k, carry):
        mlp(2 * k + 1, a1, a0)
        pl.when(k == k1)(text0)
        pl.when(k == k1 + 1)(text2)
        mlp(2 * k + 2, a0, a1)
        pl.when(k == k1)(text1)
        pl.when(k == k1 + 1)(text3)
        pl.when(k == k2)(text4)
        return carry
    lax.fori_loop(0, nf // 2 - 1, two, 0)
    mlp(jnp.int32(nf - 1), a1, a0)

    for r in range(1, NCHIP):
        r_copy(r, lax.rem(chip + NCHIP - r, NCHIP), chip).wait_recv()
    ref = tout_ref.at[pl.ds(pl.multiple_of(core * rows, 8), rows), :]
    fwd = pltpu.make_async_remote_copy(src_ref=ref, dst_ref=ref, send_sem=fssem, recv_sem=frsem,
                                       device_id={"cp": sib}, device_id_type=MESH)
    fwd.start()

    slot = get_b(jnp.int32(nf - 1))
    y = acc[...] + dot(a1[...], wb[slot])
    out_ref[...] = (h[...] + mi_ref[5:6, :] * y).astype(BF16)

    fwd.wait()
    for j in range(nj):
        for r in range(1, NCHIP):
            o_copy(j, r, chip, lax.rem(chip + r, NCHIP)).wait_send()
    for r in range(1, NCHIP):
        c = lax.rem(chip + r, NCHIP)
        p_copy(r, chip, c).wait_send()
        r_copy(r, chip, c).wait_send()


def output(o_img, image, text, o_txt, g2, flat, wp, w1, w2, twp, tw1, tw2):
    tok, d = image.shape
    txt = text.shape[0]
    ff = w1.shape[1]
    nb = 512
    nf = ff // nb
    k1, k2 = (1, 9) if nf > 8 else (0, 2)
    na = 3
    rows = txt // 2
    ft = ff // NCHIP
    nj = o_txt.shape[0]
    dma = pltpu.SemaphoreType.DMA
    flops = 2 * tok * d * (d + 2 * ff) + 2 * rows * d * (d + 2 * ft)
    return pl.pallas_call(
        functools.partial(out_kernel, (tok, txt, d, ff, k1, k2)),
        out_shape=(jax.ShapeDtypeStruct((tok, d), BF16), jax.ShapeDtypeStruct((txt, d), BF16)),
        in_specs=[ANY, ANY, ANY, VM, VM] + [VM] * 8 + [ANY] * 6,
        out_specs=(VM, VM),
        scratch_shapes=[
            pltpu.VMEM((6, d), F32), pltpu.VMEM((6, d), F32),
            pltpu.VMEM((na, d, nb), BF16), pltpu.VMEM((na, nb, d), BF16), pltpu.VMEM((na, d, nb), BF16),
            pltpu.VMEM((tok, d), BF16), pltpu.VMEM((tok, d), BF16), pltpu.VMEM((tok, d), F32), pltpu.VMEM((tok, d), BF16),
            pltpu.VMEM((tok, d), F32), pltpu.VMEM((tok, nb), BF16), pltpu.VMEM((tok, nb), BF16),
            pltpu.VMEM((rows, d), BF16), pltpu.VMEM((rows, d), BF16), pltpu.VMEM((rows, d), F32), pltpu.VMEM((rows, d), BF16),
            pltpu.VMEM((rows, ft), BF16), pltpu.VMEM((rows, d), F32), pltpu.VMEM((NCHIP, rows // NCHIP, d), F32),
            pltpu.VMEM((rows // NCHIP, d), BF16),
            dma((na,)), dma((na,)), dma((na,)), dma((3,)), dma((nj, NCHIP)), dma((nj, NCHIP)), dma((NCHIP,)), dma((NCHIP,)),
            dma((NCHIP,)), dma((NCHIP,)), dma, dma,
        ],
        compiler_params=pltpu.CompilerParams(collective_id=2, has_side_effects=True, vmem_limit_bytes=VMEM_LIMIT),
        cost_estimate=pl.CostEstimate(flops=flops, bytes_accessed=2 * d * (d + 2 * ff), transcendentals=0),
        name="out",
    )(o_img, image, text, o_txt, g2, *flat, wp, w1, w2, twp, tw1, tw2)


def rope_inputs(ids):
    d_t = HD // 8
    d_s = (HD - d_t) // 2
    widths = (d_t, d_s, d_s)
    lane = lax.broadcasted_iota(jnp.int32, (1, HD), 1)
    pos = jnp.where(lane < d_t, ids[:, 0:1], jnp.where(lane < d_t + d_s, ids[:, 1:2], ids[:, 2:3])).astype(BF16)
    omega = np.concatenate([np.repeat(THETA ** (-np.arange(0, w, 2, dtype=np.float32) / np.float32(w)), 2) for w in widths])
    return pos, jnp.asarray(omega.astype(np.float32)[None, :])


def device_fn(image, text, cond_vec, image_ids, *weights):
    (wm, bm, wqkv, bqkv, qg, kg, wp, bp, w1, b1, w2, b2) = weights[:12]
    (twm, tbm, twqkv, tbqkv, tqg, tkg, twp, tbp, tw1, tb1, tw2, tb2) = weights[12:]
    x, xt = image[0], text[0]
    pos, omega = rope_inputs(image_ids)
    o_img, o_txt, g2 = attention(x, xt, cond_vec, wm, twm, wqkv, twqkv, (bm, tbm, bqkv, tbqkv, qg, kg, tqg, tkg), pos, omega)
    image_out, text_out = output(o_img, x, xt, o_txt, g2, (bm, tbm, bp, tbp, b1, tb1, b2, tb2), wp, w1, w2, twp, tw1, tw2)
    return image_out[None], text_out[None]


def solution(mesh):
    act = P("dp", "cp", None)
    txt = P("dp", None, None)
    in_specs = (act, txt, P("dp", None), P(("dp", "cp"), None)) + (P(),) * 24
    return jax.shard_map(device_fn, mesh=mesh, in_specs=in_specs, out_specs=(act, txt), check_vma=False)
```

profile of v0, /device:TPU:0, one launch (start us, length us, event | category | flops | bytes accessed | tf_op | source)
XLA Modules:
  0.0 351.1 jit_solution(331132182431833253)
XLA Ops:
  0.6 0.8 slice_reduce_fusion.2
  1.5 0.9 select_convert_fusion.pos_ref
  2.3 233.4 %attn.1 = (bf16[384,3072]{1,0:T(8,128)(2,1)}, bf16[3,128,128]{2,1,0:T(8,128)(2,1)}, f32[16,16,128]{2,1,0:T(8,128)}) custom-call(bf16[384,3072]{1,0:T(8,128)(2,1)} %bitcast.4, bf16[256,3072]{1,0:T(8,128)(2,1)} %bitcast.6, bf16[1,3072]{1,0:T(2,128)(2,1)} %cond_ref.1, bf16[3072,18432]{1,0:T(8,128)(2,1)} %wmi_hbm.1, bf16[3072,18432]{1,0:T(8,128)(2,1)} %wmt_hbm.1, ...), custom_call_target="tpu_custom_call" | custom-call | flops 54458843136 | bytes 84934656 | tf_op jit(solution)/shard_map/attn/pallas_call | solution.py:524
  235.8 109.5 %out.1 = (bf16[384,3072]{1,0:T(8,128)(2,1)}, bf16[256,3072]{1,0:T(8,128)(2,1)}) custom-call(bf16[384,3072]{1,0:T(8,128)(2,1)} %get-tuple-element.7.o_hbm, bf16[384,3072]{1,0:T(8,128)(2,1)} %bitcast.5, bf16[256,3072]{1,0:T(8,128)(2,1)} %bitcast.7, bf16[3,128,128]{2,1,0:T(8,128)(2,1)} %get-tuple-element.8.ot_ref, f32[16,16,128]{2,1,0:T(8,128)} %get-tuple-element.9.g2_ref, ...), custom_call_target="tpu_custom_call" | custom-call | flops 70061654016 | bytes 169869312 | tf_op jit(solution)/shard_map/out/pallas_call | solution.py:816
  345.2 3.2 copy.33
  348.5 2.7 copy.34
  (1 shorter events, 0.0 us)
where the time goes:
time: 353 us; the launch traced here: 351 us
  Pallas kernels  343 us (97%)
  local copies, waits for them, and re-layouts  6.7 us (2%)
    pallas_call x1, Pallas kernels, attention(): pl.pallas_call(functools.partial(main_kernel, cfg), out_shape=(jax.ShapeD...  233 us
    pallas_call x1, Pallas kernels, output(): pl.pallas_call(functools.partial(out_kernel, (tok, txt, d, ff, k1, k2)),...  109 us

commit v1 on v0

--- a/solution.py
+++ b/solution.py
@@ -250,7 +250,7 @@
     ln_rows(xs, mi, tok)
 
     last = nj - 1
-    mir_after = min(1, last)
+    mir_after = 0
 
     def text_rows():
         load_t.wait()
@@ -258,7 +258,7 @@
         for t, kind in enumerate(KINDS):
             if t == 0:
                 start_txt(2)
-            elif nj > 1:
+            elif mir_after > 0:
                 start_own(1, t - 1)
             else:
                 start_mir(0, t - 1)
@@ -511,7 +511,7 @@
     half = tok * NCHIP
     keys = txt + 2 * half
     ck = 3200
-    mx = 2 * tok // 3
+    mx = tok // 3
     nu = tok - mx
     cfg = (tok, txt, d_in, heads, ck, mx)
     dma = pltpu.SemaphoreType.DMA
@@ -559,19 +559,21 @@
     chip, core = me // 2, me % 2
     sib = chip * 2 + (1 - core)
     rows = txt // 2
-    piece = rows // NCHIP
+    quad = 4
+    cl, zq = chip % quad, chip // quad * quad
+    piece = rows // quad
     nb = wa.shape[2]
     na = wa.shape[0]
     np_ = d // nb
     nf = ff // nb
-    ft = ff // NCHIP
+    ft = ff // quad
     nt = ft // nb
     nj = ot_ref.shape[0]
 
     def dev(c):
         return {"cp": c * 2 + core}
 
-    off = pl.multiple_of(chip * ft, nb)
+    off = pl.multiple_of(cl * ft, nb)
 
     def start_a(p):
         slot = lax.rem(p, na)
@@ -717,46 +719,58 @@
     def p_copy(r, c_src, c_dst):
         return pltpu.make_async_remote_copy(
             src_ref=part.at[pl.ds(pl.multiple_of(c_dst * piece, 8), piece), :], dst_ref=rs.at[c_src],
-            send_sem=pssem.at[r], recv_sem=prsem.at[r], device_id=dev(c_dst), device_id_type=MESH)
-
-    mine = pl.ds(pl.multiple_of(chip * piece, 8), piece)
-
-    def text0():
-        load_t.wait()
-        for j in range(nj):
-            for r in range(1, NCHIP):
-                o_copy(j, r, lax.rem(chip + NCHIP - r, NCHIP), chip).wait_recv()
-        lax.fori_loop(0, np_ // 2, tproj, 0)
-
-    def text1():
-        lax.fori_loop(np_ // 2, np_, tproj, 0)
-
-    def text2():
-        ln2(h_t, z_t, mt_ref, rows)
-        lax.fori_loop(0, nt, tfc1, 0)
-
-    def text3():
-        lax.fori_loop(0, np_, tfc2, 0)
-        for r in range(1, NCHIP):
-            p_copy(r, chip, lax.rem(chip + r, NCHIP)).start()
-        rs[chip] = part[mine, :]
+            send_sem=pssem.at[r], recv_sem=prsem.at[r], device_id=dev(zq + c_dst), device_id_type=MESH)
 
     def r_copy(r, c_src, c_dst):
         return pltpu.make_async_remote_copy(
             src_ref=row, dst_ref=tout_ref.at[pl.ds(pl.multiple_of(core * rows + c_src * piece, 8), piece), :],
-            send_sem=rssem.at[r], recv_sem=rrsem.at[r], device_id=dev(c_dst), device_id_type=MESH)
-
-    def text4():
-        for r in range(1, NCHIP):
-            p_copy(r, lax.rem(chip + NCHIP - r, NCHIP), chip).wait_recv()
-        tot = rs[0]
-        for c in range(1, NCHIP):
-            tot = tot + rs[c]
-        y = h_t[mine, :] + mt_ref[5:6, :] * (tot + lane_row(tb2_ref, 0, d))
-        row[...] = y.astype(BF16)
-        for r in range(1, NCHIP):
-            r_copy(r, chip, lax.rem(chip + r, NCHIP)).start()
-        tout_ref[pl.ds(pl.multiple_of(core * rows + chip * piece, 8), piece), :] = row[...]
+            send_sem=rssem.at[r], recv_sem=rrsem.at[r], device_id=dev(zq + c_dst), device_id_type=MESH)
+
+    mine = pl.ds(pl.multiple_of(cl * piece, 8), piece)
+    n1, n2, n3 = np_ // 2, np_ // 2 + nt // 2, np_ + nt // 2
+
+    def text_step(s):
+        @pl.when(s == 0)
+        def _():
+            load_t.wait()
+            for j in range(nj):
+                for r in range(1, NCHIP):
+                    o_copy(j, r, lax.rem(chip + NCHIP - r, NCHIP), chip).wait_recv()
+
+        @pl.when((s >= 0) & (s < n1))
+        def _():
+            lax.fori_loop(2 * s, 2 * s + 2, tproj, 0)
+
+        @pl.when(s == n1)
+        def _():
+            ln2(h_t, z_t, mt_ref, rows)
+
+        @pl.when((s >= n1) & (s < n2))
+        def _():
+            lax.fori_loop(2 * (s - n1), 2 * (s - n1) + 2, tfc1, 0)
+
+        @pl.when((s >= n2) & (s < n3))
+        def _():
+            lax.fori_loop(2 * (s - n2), 2 * (s - n2) + 2, tfc2, 0)
+
+        @pl.when(s == n3 - 1)
+        def _():
+            for r in range(1, quad):
+                p_copy(r, cl, lax.rem(cl + r, quad)).start()
+            rs[cl] = part[mine, :]
+
+        @pl.when(s == k2)
+        def _():
+            for r in range(1, quad):
+                p_copy(r, lax.rem(cl + quad - r, quad), cl).wait_recv()
+            tot = rs[0]
+            for c in range(1, quad):
+                tot = tot + rs[c]
+            y = h_t[mine, :] + mt_ref[5:6, :] * (tot + lane_row(tb2_ref, 0, d))
+            row[...] = y.astype(BF16)
+            for r in range(1, quad):
+                r_copy(r, cl, lax.rem(cl + r, quad)).start()
+            tout_ref[pl.ds(pl.multiple_of(core * rows + cl * piece, 8), piece), :] = row[...]
 
     def mlp(i, a_new, a_old):
         slot_b = get_b(i - 1)
@@ -769,18 +783,15 @@
 
     def two(k, carry):
         mlp(2 * k + 1, a1, a0)
-        pl.when(k == k1)(text0)
-        pl.when(k == k1 + 1)(text2)
+        text_step(2 * k - k1)
         mlp(2 * k + 2, a0, a1)
-        pl.when(k == k1)(text1)
-        pl.when(k == k1 + 1)(text3)
-        pl.when(k == k2)(text4)
+        text_step(2 * k + 1 - k1)
         return carry
     lax.fori_loop(0, nf // 2 - 1, two, 0)
     mlp(jnp.int32(nf - 1), a1, a0)
 
-    for r in range(1, NCHIP):
-        r_copy(r, lax.rem(chip + NCHIP - r, NCHIP), chip).wait_recv()
+    for r in range(1, quad):
+        r_copy(r, lax.rem(cl + quad - r, quad), cl).wait_recv()
     ref = tout_ref.at[pl.ds(pl.multiple_of(core * rows, 8), rows), :]
     fwd = pltpu.make_async_remote_copy(src_ref=ref, dst_ref=ref, send_sem=fssem, recv_sem=frsem,
                                        device_id={"cp": sib}, device_id_type=MESH)
@@ -794,10 +805,10 @@
     for j in range(nj):
         for r in range(1, NCHIP):
             o_copy(j, r, chip, lax.rem(chip + r, NCHIP)).wait_send()
-    for r in range(1, NCHIP):
-        c = lax.rem(chip + r, NCHIP)
-        p_copy(r, chip, c).wait_send()
-        r_copy(r, chip, c).wait_send()
+    for r in range(1, quad):
+        c = lax.rem(cl + r, quad)
+        p_copy(r, cl, c).wait_send()
+        r_copy(r, cl, c).wait_send()
 
 
 def output(o_img, image, text, o_txt, g2, flat, wp, w1, w2, twp, tw1, tw2):
@@ -806,10 +817,10 @@
     ff = w1.shape[1]
     nb = 512
     nf = ff // nb
-    k1, k2 = (1, 9) if nf > 8 else (0, 2)
+    k1, k2 = (2, 16) if nf > 8 else (0, 5)
     na = 3
     rows = txt // 2
-    ft = ff // NCHIP
+    ft = ff // 4
     nj = o_txt.shape[0]
     dma = pltpu.SemaphoreType.DMA
     flops = 2 * tok * d * (d + 2 * ff) + 2 * rows * d * (d + 2 * ft)
@@ -824,8 +835,8 @@
             pltpu.VMEM((tok, d), BF16), pltpu.VMEM((tok, d), BF16), pltpu.VMEM((tok, d), F32), pltpu.VMEM((tok, d), BF16),
             pltpu.VMEM((tok, d), F32), pltpu.VMEM((tok, nb), BF16), pltpu.VMEM((tok, nb), BF16),
             pltpu.VMEM((rows, d), BF16), pltpu.VMEM((rows, d), BF16), pltpu.VMEM((rows, d), F32), pltpu.VMEM((rows, d), BF16),
-            pltpu.VMEM((rows, ft), BF16), pltpu.VMEM((rows, d), F32), pltpu.VMEM((NCHIP, rows // NCHIP, d), F32),
-            pltpu.VMEM((rows // NCHIP, d), BF16),
+            pltpu.VMEM((rows, ft), BF16), pltpu.VMEM((rows, d), F32), pltpu.VMEM((4, rows // 4, d), F32),
+            pltpu.VMEM((rows // 4, d), BF16),
             dma((na,)), dma((na,)), dma((na,)), dma((3,)), dma((nj, NCHIP)), dma((nj, NCHIP)), dma((NCHIP,)), dma((NCHIP,)),
             dma((NCHIP,)), dma((NCHIP,)), dma, dma,
         ],

time: 353 us -> 320 us (0.907)
  Pallas kernels: 343 us -> 311 us
    pallas_call x1, Pallas kernels: 233 us -> 201 us  [attention(): pl.pallas_call(functools.partial(main_kernel, cfg), out_shape=(jax.ShapeD...]
where the time goes in v1:
time: 320 us; the launch traced here: 319 us
  Pallas kernels  311 us (97%)
  local copies, waits for them, and re-layouts  6.7 us (2%)
    pallas_call x1, Pallas kernels, attention(): pl.pallas_call(functools.partial(main_kernel, cfg), out_shape=(jax.ShapeD...  201 us
    pallas_call x1, Pallas kernels, output(): pl.pallas_call(functools.partial(out_kernel, (tok, txt, d, ff, k1, k2)),...  110 us

profile of v1, /device:TPU:0, one launch (start us, length us, event | category | flops | bytes accessed | tf_op | source)
XLA Modules:
  0.0 318.9 jit_solution(1268969594964179766)
XLA Ops:
  0.6 0.8 slice_reduce_fusion.2
  1.5 0.9 select_convert_fusion.pos_ref
  2.3 200.5 %attn.1 = (bf16[384,3072]{1,0:T(8,128)(2,1)}, bf16[3,128,128]{2,1,0:T(8,128)(2,1)}, f32[16,16,128]{2,1,0:T(8,128)}) custom-call(bf16[384,3072]{1,0:T(8,128)(2,1)} %bitcast.4, bf16[256,3072]{1,0:T(8,128)(2,1)} %bitcast.6, bf16[1,3072]{1,0:T(2,128)(2,1)} %cond_ref.1, bf16[3072,18432]{1,0:T(8,128)(2,1)} %wmi_hbm.1, bf16[3072,18432]{1,0:T(8,128)(2,1)} %wmt_hbm.1, ...), custom_call_target="tpu_custom_call" | custom-call | flops 54458843136 | bytes 84934656 | tf_op jit(solution)/shard_map/attn/pallas_call | solution.py:524
  202.9 110.2 %out.1 = (bf16[384,3072]{1,0:T(8,128)(2,1)}, bf16[256,3072]{1,0:T(8,128)(2,1)}) custom-call(bf16[384,3072]{1,0:T(8,128)(2,1)} %get-tuple-element.7.o_hbm, bf16[384,3072]{1,0:T(8,128)(2,1)} %bitcast.5, bf16[256,3072]{1,0:T(8,128)(2,1)} %bitcast.7, bf16[3,128,128]{2,1,0:T(8,128)(2,1)} %get-tuple-element.8.ot_ref, f32[16,16,128]{2,1,0:T(8,128)} %get-tuple-element.9.g2_ref, ...), custom_call_target="tpu_custom_call" | custom-call | flops 72477573120 | bytes 169869312 | tf_op jit(solution)/shard_map/out/pallas_call | solution.py:827
  313.1 3.2 %copy.33 = bf16[1,384,3072]{2,1,0:T(8,128)(2,1)} copy(bf16[1,384,3072]{2,1,0:T(8,128)(2,1)} %bitcast.8) | data formatting | bytes 4718592
  316.3 2.7 copy.34
  (1 shorter events, 0.0 us)

commit v2 on v1

--- a/solution.py
+++ b/solution.py
@@ -120,8 +120,6 @@
 
     start("mod", 0, -1, 0)
     start("mod", 1, -1, 1)
-    load_x.start()
-    load_t.start()
 
     c = cond_ref[...].astype(F32)
     act = (c * jax.nn.sigmoid(c)).astype(BF16)
@@ -139,10 +137,14 @@
             device_id={"cp": lax.rem(me + r, NDEV)}, device_id_type=MESH) for r in range(1, NDEV)]
 
     mine1[...] = jnp.zeros_like(mine1)
+    slot = wait("mod", 0, -1, 0)
+    load_x.start()
+    mod_rows(slot, mine1, 0)
+    slot = wait("mod", 1, -1, 1)
     start_own(0, 0)
-    mod_rows(wait("mod", 0, -1, 0), mine1, 0)
     start_own(0, 1)
-    mod_rows(wait("mod", 1, -1, 1), mine1, per)
+    load_t.start()
+    mod_rows(slot, mine1, per)
     pl.semaphore_wait(barrier, NDEV - 1)
     gath1 = spread(mine1, g1, 0)
     for cp in gath1:
@@ -172,7 +174,7 @@
                 at = (slice(col // d_in, col // d_in + 1), slice(col % d_in, col % d_in + 128))
                 m[at] = m[at] + g1[dv, b * per + r:b * per + r + 1, :]
 
-    rb = 16
+    rb = 32
 
     def ln_rows(ref, m_ref, n):
         shift = m_ref[0:1, :]
@@ -641,11 +643,6 @@
     load_x.start()
     for p in range(1, na - 1):
         start_a(jnp.int32(p))
-    load_t.start()
-    for p in range(na - 1):
-        start_b(jnp.int32(p))
-    for p in range(na - 1):
-        start_c(jnp.int32(p))
 
     barrier = pltpu.get_barrier_semaphore()
     for r in range(1, NCHIP):
@@ -679,14 +676,27 @@
     def proj(p, carry):
         slot = get_a(p)
         sl = pl.ds(pl.multiple_of(p * nb, nb), nb)
+
+        @pl.when(p == 0)
+        def _():
+            load_t.start()
+
+        @pl.when((p > 0) & (p < na))
+        def _():
+            start_b(p - 1)
+
+        @pl.when((p >= na) & (p < 2 * na - 1))
+        def _():
+            start_c(p - na)
         y = dot(o[...], wa[slot]) + lane_row(bp_ref, pl.multiple_of(p * nb, nb), nb)
         h[:, sl] = x[:, sl].astype(F32) + mi_ref[2:3, sl] * y
+        acc[:, sl] = jnp.broadcast_to(lane_row(b2_ref, pl.multiple_of(p * nb, nb), nb), (tok, nb))
         return carry
     lax.fori_loop(0, np_, proj, 0)
 
     def ln2(src, dst, m_ref, n):
         shift, scale = m_ref[3:4, :], 1.0 + m_ref[4:5, :]
-        rb = 16
+        rb = 32
 
         def body(i, carry):
             r = pl.ds(pl.multiple_of(i * rb, rb), rb)
@@ -695,7 +705,6 @@
         lax.fori_loop(0, n // rb, body, 0)
 
     ln2(h, z, mi_ref, tok)
-    acc[...] = jnp.broadcast_to(lane_row(b2_ref, 0, d), acc.shape)
 
     def tproj(p, carry):
         slot = get_c(p)
@@ -775,8 +784,12 @@
     def mlp(i, a_new, a_old):
         slot_b = get_b(i - 1)
         slot_a = get_a(np_ + i)
-        a_new[...] = gelu(dot(z[...], wa[slot_a]) + lane_row(b1_ref, pl.multiple_of(i * nb, nb), nb)).astype(BF16)
-        acc[...] += dot(a_old[...], wb[slot_b])
+        hn, hd = nb // 2, d // 2
+        for s in range(2):
+            c1, c2 = slice(s * hn, (s + 1) * hn), slice(s * hd, (s + 1) * hd)
+            b1 = lane_row(b1_ref, pl.multiple_of(i * nb + s * hn, hn), hn)
+            a_new[:, c1] = gelu(dot(z[...], wa[slot_a, :, c1]) + b1).astype(BF16)
+            acc[:, c2] += dot(a_old[...], wb[slot_b, :, c2])
 
     slot = get_a(jnp.int32(np_))
     a0[...] = gelu(dot(z[...], wa[slot]) + lane_row(b1_ref, 0, nb)).astype(BF16)
@@ -846,6 +859,37 @@
     )(o_img, image, text, o_txt, g2, *flat, wp, w1, w2, twp, tw1, tw2)
 
 
+def pass_kernel(parts, a_hbm, b_hbm, oa_hbm, ob_hbm, a, b, isem, osem):
+    moves = []
+    for k, (src, dst, buf) in enumerate(((a_hbm, oa_hbm, a), (b_hbm, ob_hbm, b))):
+        n = src.shape[0] // parts
+        for i in range(parts):
+            sl = pl.ds(i * n, n)
+            moves.append((pltpu.make_async_copy(src.at[sl, :], buf.at[sl, :], isem.at[k, i]),
+                          pltpu.make_async_copy(buf.at[sl, :], dst.at[sl, :], osem.at[k, i])))
+    for load, _ in moves:
+        load.start()
+    for load, store in moves:
+        load.wait()
+        store.start()
+    for _, store in moves:
+        store.wait()
+
+
+def pass_results(a, b):
+    parts = 4
+    dma = pltpu.SemaphoreType.DMA
+    return pl.pallas_call(
+        functools.partial(pass_kernel, parts),
+        out_shape=(jax.ShapeDtypeStruct(a.shape, a.dtype), jax.ShapeDtypeStruct(b.shape, b.dtype)),
+        in_specs=[ANY, ANY],
+        out_specs=(ANY, ANY),
+        scratch_shapes=[pltpu.VMEM(a.shape, a.dtype), pltpu.VMEM(b.shape, b.dtype), dma((2, parts)), dma((2, parts))],
+        compiler_params=pltpu.CompilerParams(vmem_limit_bytes=VMEM_LIMIT),
+        name="results",
+    )(a, b)
+
+
 def rope_inputs(ids):
     d_t = HD // 8
     d_s = (HD - d_t) // 2
@@ -863,6 +907,7 @@
     pos, omega = rope_inputs(image_ids)
     o_img, o_txt, g2 = attention(x, xt, cond_vec, wm, twm, wqkv, twqkv, (bm, tbm, bqkv, tbqkv, qg, kg, tqg, tkg), pos, omega)
     image_out, text_out = output(o_img, x, xt, o_txt, g2, (bm, tbm, bp, tbp, b1, tb1, b2, tb2), wp, w1, w2, twp, tw1, tw2)
+    image_out, text_out = pass_results(image_out, text_out)
     return image_out[None], text_out[None]
 
 

time: 320 us -> 312 us (0.975)
  local copies, waits for them, and re-layouts: 6.7 us -> 0.83 us
    unnamed x2 -> x0, local copies, waits for them, and re-layouts: 5.87 us -> none
    pallas_call x1, Pallas kernels: 110 us -> 106 us  [output(): pl.pallas_call(functools.partial(out_kernel, (tok, txt, d, ff, k1, k2)),...]
    pallas_call x0 -> x1, Pallas kernels: none -> 3.21 us  [pass_results(): pl.pallas_call(functools.partial(pass_kernel, parts), out_shape=(jax.Shap...]
where the time goes in v2:
time: 312 us
  Pallas kernels  310 us (99%)
    pallas_call x1, Pallas kernels, attention(): pl.pallas_call(functools.partial(main_kernel, cfg), out_shape=(jax.ShapeD...  200 us
    pallas_call x1, Pallas kernels, output(): pl.pallas_call(functools.partial(out_kernel, (tok, txt, d, ff, k1, k2)),...  106 us

profile of v2, /device:TPU:0, one launch (start us, length us, event | category | flops | bytes accessed | tf_op | source)
XLA Modules:
  0.0 312.1 jit_solution(13015317072233173994)
XLA Ops:
  0.6 0.8 slice_reduce_fusion.2
  1.5 0.9 select_convert_fusion.pos_ref
  2.3 200.0 %attn.1 = (bf16[384,3072]{1,0:T(8,128)(2,1)}, bf16[3,128,128]{2,1,0:T(8,128)(2,1)}, f32[16,16,128]{2,1,0:T(8,128)}) custom-call(bf16[384,3072]{1,0:T(8,128)(2,1)} %bitcast.4, bf16[256,3072]{1,0:T(8,128)(2,1)} %bitcast.6, bf16[1,3072]{1,0:T(2,128)(2,1)} %cond_ref.1, bf16[3072,18432]{1,0:T(8,128)(2,1)} %wmi_hbm.1, bf16[3072,18432]{1,0:T(8,128)(2,1)} %wmt_hbm.1, ...), custom_call_target="tpu_custom_call" | custom-call | flops 54458843136 | bytes 84934656 | tf_op jit(solution)/shard_map/attn/pallas_call | solution.py:526
  202.3 106.3 %out.1 = (bf16[384,3072]{1,0:T(8,128)(2,1)}, bf16[256,3072]{1,0:T(8,128)(2,1)}) custom-call(bf16[384,3072]{1,0:T(8,128)(2,1)} %get-tuple-element.9.o_hbm, bf16[384,3072]{1,0:T(8,128)(2,1)} %bitcast.5, bf16[256,3072]{1,0:T(8,128)(2,1)} %bitcast.7, bf16[3,128,128]{2,1,0:T(8,128)(2,1)} %get-tuple-element.10.ot_ref, f32[16,16,128]{2,1,0:T(8,128)} %get-tuple-element.11.g2_ref, ...), custom_call_target="tpu_custom_call" | custom-call | flops 72477573120 | bytes 169869312 | tf_op jit(solution)/shard_map/out/pallas_call | solution.py:840
  308.7 3.2 %results.1 = (bf16[384,3072]{1,0:T(8,128)(2,1)}, bf16[256,3072]{1,0:T(8,128)(2,1)}) custom-call(bf16[384,3072]{1,0:T(8,128)(2,1)} %get-tuple-element.12.a_hbm, bf16[256,3072]{1,0:T(8,128)(2,1)} %get-tuple-element.13.b_hbm), custom_call_target="tpu_custom_call" | custom-call | tf_op jit(solution)/shard_map/results/pallas_call | solution.py:882
  (1 shorter events, 0.0 us)

commit v3 on v2

--- a/solution.py
+++ b/solution.py
@@ -72,10 +72,13 @@
     load_x = pltpu.make_async_copy(x_hbm, xs, xsem.at[0])
     load_t = pltpu.make_async_copy(xt_hbm, xt, xsem.at[1])
 
-    def x_copy():
+    early = 16
+
+    def x_copy(part):
+        lo, n = ((0, early), (early, mx - early))[part]
         return pltpu.make_async_remote_copy(
-            src_ref=x_hbm.at[pl.ds(nu, mx), :], dst_ref=xm, send_sem=msend.at[0], recv_sem=mrecv.at[0],
-            device_id=dev(mirror_chip), device_id_type=MESH)
+            src_ref=x_hbm.at[pl.ds(nu + lo, n), :], dst_ref=xm.at[pl.ds(lo, n), :], send_sem=msend.at[2 * part],
+            recv_sem=mrecv.at[2 * part], device_id=dev(mirror_chip), device_id_type=MESH)
 
     def pos_copy():
         return pltpu.make_async_remote_copy(
@@ -137,6 +140,8 @@
             device_id={"cp": lax.rem(me + r, NDEV)}, device_id_type=MESH) for r in range(1, NDEV)]
 
     mine1[...] = jnp.zeros_like(mine1)
+    pl.semaphore_wait(barrier, NDEV - 1)
+    x_copy(0).start()
     slot = wait("mod", 0, -1, 0)
     load_x.start()
     mod_rows(slot, mine1, 0)
@@ -145,12 +150,11 @@
     start_own(0, 1)
     load_t.start()
     mod_rows(slot, mine1, per)
-    pl.semaphore_wait(barrier, NDEV - 1)
     gath1 = spread(mine1, g1, 0)
     for cp in gath1:
         cp.start()
     pos_copy().start()
-    x_copy().start()
+    x_copy(1).start()
     g1[me] = mine1[...]
 
     def tables(pos, n, cos_t, se_t, so_t):
@@ -279,7 +283,8 @@
     def mirror_rows():
         pos_copy().wait_recv()
         tables(posm[...], mx, cos_m, se_m, so_m)
-        x_copy().wait_recv()
+        for part in range(2):
+            x_copy(part).wait_recv()
         ln_rows(xm, mi, mx)
 
         lax.fori_loop(0, nj, mir_pass, 0)
@@ -360,7 +365,6 @@
     qt = 256
     ntile = (txt + half) // qt
     group = 2 * tok // qt
-    ngroup = NCHIP // 2
 
     def to_sibling(kind, j):
         ref = (kb.at[j, pl.ds(pl.multiple_of(txt + core * half, 128), half)] if kind == 1
@@ -377,9 +381,14 @@
             if kind != 0:
                 to_sibling(kind, j).start()
 
+    def plane_of(g):
+        p = (chip // 2) % 2
+        same = (g == 0) | (g == 3)
+        return jnp.where(g < 2, 1 - zh, zh) * 2 + jnp.where(same, p, 1 - p)
+
     def tile_start(t):
         g = (t - 1) // group
-        plane = lax.rem(chip // 2 + 1 + g, ngroup)
+        plane = plane_of(g)
         row = txt + plane * (2 * tok) + lax.rem(t - 1, group) * qt
         return pl.multiple_of(jnp.where(t == 0, 0, row), 128)
 
@@ -412,7 +421,7 @@
         return pltpu.make_async_copy(src, dst, ossem.at[j, chip])
 
     def o_send(j, g):
-        plane = lax.rem(chip // 2 + 1 + g, ngroup)
+        plane = plane_of(g)
         for y in range(2):
             c = plane * 2 + y
 
@@ -487,7 +496,8 @@
 
     for cp in gath2:
         cp.wait()
-    x_copy().wait_send()
+    for part in range(2):
+        x_copy(part).wait_send()
     pos_copy().wait_send()
 
     def drain(j, carry):
@@ -539,7 +549,7 @@
             pltpu.VMEM((NDEV, r1, 128), F32), pltpu.VMEM((r1, 128), F32), pltpu.VMEM((r2, 128), F32),
             pltpu.VMEM((keys, 256), F32), pltpu.VMEM((keys, 256), F32), pltpu.VMEM((8, 256), F32), pltpu.VMEM((8, 256), F32),
             pltpu.VMEM((nj, half, HD), BF16), pltpu.VMEM((txt, HD), BF16),
-            dma((2,)), dma((3, max(nj, 1))), dma((2,)), dma((2,)), dma((2, NDEV)), dma((2, NDEV)),
+            dma((2,)), dma((3, max(nj, 1))), dma((3,)), dma((3,)), dma((2, NDEV)), dma((2, NDEV)),
             dma((3, 3, nj, 4)), dma((3, 3, nj, 4)), dma((2, nj)), dma((2, nj)), dma((nj, NCHIP)), dma((nj, NCHIP)),
         ],
         compiler_params=pltpu.CompilerParams(collective_id=1, has_side_effects=True, vmem_limit_bytes=VMEM_LIMIT),

time: 312 us -> 311 us (level)
    pallas_call x1, Pallas kernels: 106 us -> 102 us  [output(): pl.pallas_call(functools.partial(out_kernel, (tok, txt, d, ff, k1, k2)),...]
where the time goes in v3:
time: 311 us
  Pallas kernels  308 us (99%)
    pallas_call x1, Pallas kernels, attention(): pl.pallas_call(functools.partial(main_kernel, cfg), out_shape=(jax.ShapeD...  203 us
    pallas_call x1, Pallas kernels, output(): pl.pallas_call(functools.partial(out_kernel, (tok, txt, d, ff, k1, k2)),...  102 us

profile of v3, /device:TPU:0, one launch (start us, length us, event | category | flops | bytes accessed | tf_op | source)
XLA Modules:
  0.0 310.6 jit_solution(2695743555894874016)
XLA Ops:
  0.6 0.8 slice_reduce_fusion.2
  1.5 0.9 select_convert_fusion.pos_ref
  2.3 202.6 %attn.1 = (bf16[384,3072]{1,0:T(8,128)(2,1)}, bf16[3,128,128]{2,1,0:T(8,128)(2,1)}, f32[16,16,128]{2,1,0:T(8,128)}) custom-call(bf16[384,3072]{1,0:T(8,128)(2,1)} %bitcast.4, bf16[256,3072]{1,0:T(8,128)(2,1)} %bitcast.6, bf16[1,3072]{1,0:T(2,128)(2,1)} %cond_ref.1, bf16[3072,18432]{1,0:T(8,128)(2,1)} %wmi_hbm.1, bf16[3072,18432]{1,0:T(8,128)(2,1)} %wmt_hbm.1, ...), custom_call_target="tpu_custom_call" | custom-call | flops 54458843136 | bytes 84934656 | tf_op jit(solution)/shard_map/attn/pallas_call | solution.py:536
  204.9 102.3 %out.1 = (bf16[384,3072]{1,0:T(8,128)(2,1)}, bf16[256,3072]{1,0:T(8,128)(2,1)}) custom-call(bf16[384,3072]{1,0:T(8,128)(2,1)} %get-tuple-element.9.o_hbm, bf16[384,3072]{1,0:T(8,128)(2,1)} %bitcast.5, bf16[256,3072]{1,0:T(8,128)(2,1)} %bitcast.7, bf16[3,128,128]{2,1,0:T(8,128)(2,1)} %get-tuple-element.10.ot_ref, f32[16,16,128]{2,1,0:T(8,128)} %get-tuple-element.11.g2_ref, ...), custom_call_target="tpu_custom_call" | custom-call | flops 72477573120 | bytes 169869312 | tf_op jit(solution)/shard_map/out/pallas_call | solution.py:850
  307.2 3.2 %results.1 = (bf16[384,3072]{1,0:T(8,128)(2,1)}, bf16[256,3072]{1,0:T(8,128)(2,1)}) custom-call(bf16[384,3072]{1,0:T(8,128)(2,1)} %get-tuple-element.12.a_hbm, bf16[256,3072]{1,0:T(8,128)(2,1)} %get-tuple-element.13.b_hbm), custom_call_target="tpu_custom_call" | custom-call | tf_op jit(solution)/shard_map/results/pallas_call | solution.py:892
  (1 shorter events, 0.0 us)
